TPU v7x, 32 devices: a whole 2x2x4 slice. The times are simulated.
32 devices in a mesh: pole: 2 (over y), prow: 4 (over z), pcol: 4 (over x, core).
Axes of the slice: x: 2, y: 2, z: 4, core: 2. Of those that a mesh axis runs over, the one named last changes fastest.
Arguments:
- ainv_anc: bfloat16 [2, 4096, 2048], P(None, ('pole', 'prow'), 'pcol'), parts along dimension 1, may hold values from -6 to 6
- panel: bfloat16 [2, 8, 1024, 256], P(None, 'pole', ('pcol', 'prow')), parts along dimension 1, may hold values from -6 to 6
- u_inv: bfloat16 [2, 8, 256, 256], P(None, 'pole'), parts along dimension 1, may hold values from -0.01171875 to 0.01171875
- k_inv: float32 [2, 8, 256, 256], P(None, ('pole', 'pcol')), parts along dimension 1, may hold values from -6 to 6
- structure: int32 [4, 4], replicated, may hold values from -1 to 7, as said below
Outputs:
- sel_inv: float32 [2, 4096, 1024], P(None, ('pole', 'prow'), 'pcol'), parts along dimension 1
- diag_inv: float32 [2, 8, 256, 256], P(None, ('pole', 'pcol')), parts along dimension 1
There are 2 independent parts, one for each index of `pole`. A program takes and returns all parts, laid end to end along the dimension named above; an argument that names none is the same for every part. Nothing has to cross between parts.
Inputs may be any that keep to these rules, and one draw needn't show every extreme that they name: `structure`: slots g * 1 to (g + 1) * 1 - 1 of row k hold distinct blocks of g * 2 to (g + 1) * 2 - 1 in rising order, followed by -1 for empty slots; each such group of each row holds at least one block, and for every g some row fills all 1 slots of group g.
All inputs are finite; a program needn't handle non-finite values.
Results may differ from a plain program's by a relative error of at most 0.005.
Values may be sent and summed in bfloat16 or wider, within the bound.
No kernel may reach another device: no remote copies, remote signals or barrier semaphores. Data moves between devices by JAX's collectives and lax.ppermute only.
A program may use at most 128 MiB of HBM per device.

v0:
```python
import jax
import jax.numpy as jnp
from jax import lax
from jax.sharding import PartitionSpec as P


def complex_quad(z_part, s_part):
    highest = lax.Precision.HIGHEST

    def single(left, right):
        return jnp.einsum("kra,rkb->kab", left, right, precision=highest)

    real = single(z_part[0], s_part[0]) - single(z_part[1], s_part[1])
    imag = single(z_part[0], s_part[1]) + single(z_part[1], s_part[0])
    return jnp.stack([real, imag])


def local(ainv_anc, panel, u_inv, k_inv, structure):
    block_width = u_inv.shape[-1]
    total_k = u_inv.shape[1]
    own_k = k_inv.shape[1]
    n_cols = lax.axis_size("pcol")
    row_here = lax.axis_index("prow")
    col_here = lax.axis_index("pcol")
    row_blocks = ainv_anc.shape[1] // block_width
    group_blocks = ainv_anc.shape[2] // block_width
    group_slots = structure.shape[1] // n_cols
    rows_all = row_blocks * block_width
    col_struct = lax.dynamic_slice_in_dim(structure, col_here * group_slots, group_slots, 1)
    slot_live = col_struct >= 0
    slot_pos = col_struct - col_here * group_blocks
    first_block = row_here * row_blocks
    target = first_block + jnp.arange(row_blocks, dtype=jnp.int32)
    rows_in = lax.all_gather(panel, "prow", axis=2, tiled=True)

    def single(left, right):
        return jnp.einsum("knb,kbc->knc", left, right, preferred_element_type=jnp.float32)

    real = single(rows_in[0], u_inv[0]) - single(rows_in[1], u_inv[1])
    imag = single(rows_in[0], u_inv[1]) + single(rows_in[1], u_inv[0])
    placed = jnp.stack([real, imag]).astype(jnp.bfloat16)
    placed = placed.reshape(2, total_k, group_slots, block_width, block_width)
    placed = jnp.where(slot_live[None, :, :, None, None], placed, jnp.zeros((), jnp.bfloat16))
    block_ids = jnp.arange(group_blocks, dtype=jnp.int32)
    pick_table = (slot_pos[:, :, None] == block_ids[None, None, :]).astype(jnp.bfloat16)
    ainv_blocks = ainv_anc.reshape(2, rows_all, group_blocks, block_width)

    def one_node(items):
        table_k, rows_k = items
        picked = jnp.einsum(
            "sg,cigw->cisw", table_k, ainv_blocks, preferred_element_type=jnp.float32
        )
        picked = picked.astype(jnp.bfloat16).reshape(2, rows_all, group_slots * block_width)
        right = rows_k.reshape(2, group_slots * block_width, block_width)
        real = jnp.dot(picked[0], right[0], preferred_element_type=jnp.float32) - jnp.dot(
            picked[1], right[1], preferred_element_type=jnp.float32
        )
        imag = jnp.dot(picked[0], right[1], preferred_element_type=jnp.float32) + jnp.dot(
            picked[1], right[0], preferred_element_type=jnp.float32
        )
        return jnp.stack([real, imag])

    per_node = lax.map(one_node, (pick_table, jnp.moveaxis(placed, 1, 0)))
    partial_value = jnp.transpose(per_node, (1, 2, 0, 3))
    row_table = (col_struct[:, None, :] == target[None, :, None]).astype(jnp.bfloat16)
    z_rows = jnp.einsum("kts,ckswb->cktwb", row_table, placed, preferred_element_type=jnp.float32)
    z_rows = z_rows.astype(jnp.bfloat16).reshape(2, total_k, rows_all, block_width)
    summed = lax.psum_scatter(
        partial_value.reshape(2, rows_all, total_k * block_width),
        "pcol",
        scatter_dimension=2,
        tiled=True,
    )
    own_struct = lax.dynamic_slice_in_dim(structure, col_here * own_k, own_k, 0)
    member = jnp.any(own_struct[:, :, None] == target[None, None, :], axis=1)
    selected = -summed.reshape(2, row_blocks, block_width, own_k, block_width)
    selected = jnp.where(member.T[None, :, None, :, None], selected, 0.0)
    sel_inv = selected.reshape(2, rows_all, own_k * block_width)
    received = lax.all_to_all(z_rows, "pcol", split_axis=1, concat_axis=1, tiled=True)
    z_own = (
        received.astype(jnp.float32).reshape(2, n_cols, own_k, rows_all, block_width).sum(axis=1)
    )
    quad_term = complex_quad(z_own, selected.reshape(2, rows_all, own_k, block_width))
    total_sum = lax.psum(quad_term, "prow")
    diag_inv = k_inv - total_sum
    return (sel_inv, diag_inv)


def solution(mesh):
    placed = (
        P(None, ("pole", "prow"), "pcol"),
        P(None, "pole", ("pcol", "prow"), None),
        P(None, "pole", None, None),
        P(None, ("pole", "pcol"), None, None),
        P(),
    )
    return jax.shard_map(
        local,
        mesh=mesh,
        in_specs=placed,
        out_specs=(P(None, ("pole", "prow"), "pcol"), P(None, ("pole", "pcol"), None, None)),
        check_vma=False,
    )
```

profile of v0, /device:TPU:0, one launch (start us, length us, event | category | flops | bytes accessed | tf_op | source)
XLA Modules:
  0.0 170.8 jit_solution(10218093751577018464)
XLA Ops:
  7.2 0.7 all-gather.2.cloned.1.call-update
  8.0 1.3 reshape.276
  9.3 0.9 compare_reduce_fusion
  10.2 0.9 dynamic-slice_reduce_fusion
  11.2 29.1 %all-gather.2.cloned.1.call-done = bf16[2,4,256,256]{3,2,1,0:T(8,128)(2,1)} async-done(((bf16[2,4,64,256]{3,2,1,0:T(8,128)(2,1)}), bf16[2,4,256,256]{3,2,1,0:T(8,128)(2,1)}) %all-gather.2.cloned.1.call-update) | async-done | bytes 1048592 | tf_op jit(solution)/shard_map/all_gather | solution.py:34
  40.3 1.6 fusion.13
  41.9 1.3 fusion.17
  43.3 0.3 fusion.9
  44.1 13.4 %while.10 = (s32[]{:T(128)}, f32[4,2,512,256]{3,2,1,0:T(8,128)}, bf16[4,1,2]{2,1,0:T(2,128)(2,1)S(1)}, bf16[2,512,2,256]{3,2,1,0:T(2,128)(2,1)S(1)}, bf16[4,2,1,256,256]{4,3,0,2,1:T(8,128)(2,1)S(1)}, /*index=5*/s32[]{:T(128)}) while((s32[]{:T(128)}, f32[4,2,512,256]{3,2,1,0:T(8,128)}, bf16[4,1,2]{2,1,0:T(2,128)(2,1)S(1)}, ...), condition=%wide.region_2.3_spmd, body=%wide.region_1.2_spmd.sunk | while | flops 270008320 | bytes 9962073 | solution.py:63
  44.1 1.2 fusion.42
  46.4 1.0 fusion.47
  47.4 1.2 fusion.42
  49.7 1.1 fusion.47
  50.8 1.2 fusion.42
  53.1 1.1 fusion.47
  54.2 1.2 fusion.42
  56.4 1.0 fusion.47
  57.5 4.8 %copy.21 = f32[4,2,64,8,256]{4,3,0,2,1:T(8,128)} copy(f32[4,2,64,8,256]{4,3,2,1,0:T(8,128)} %bitcast.135) | data formatting | bytes 8388608 | tf_op jit(solution)/shard_map/reshape | solution.py:69
  62.5 0.5 multiply_convert_fusion
  63.0 1.5 copy.17
  64.5 3.8 %all-to-all-start = ((bf16[2,4,512,256]{3,2,0,1:T(8,128)(2,1)}), bf16[2,4,512,256]{3,2,0,1:T(8,128)(2,1)S(1)}, u32[]{:S(2)}, u32[]{:S(2)}) async-start(bf16[2,4,512,256]{3,2,0,1:T(8,128)(2,1)} %copy.17), calls=%async_computation.1 | async-start | bytes 4194304 | tf_op jit(solution)/shard_map/all_to_all | solution.py:79
  68.3 0.7 dynamic-slice_bitcast_fusion.1
  69.2 36.9 %all-to-all-done = bf16[2,4,512,256]{3,2,0,1:T(8,128)(2,1)S(1)} async-done(((bf16[2,4,512,256]{3,2,0,1:T(8,128)(2,1)}), bf16[2,4,512,256]{3,2,0,1:T(8,128)(2,1)S(1)}, u32[]{:S(2)}, u32[]{:S(2)}) %all-to-all-start) | async-done | bytes 2097184 | tf_op jit(solution)/shard_map/all_to_all | solution.py:79
  106.4 11.5 %reduce-scatter.2.cloned.1.call-done = f32[2,512,256]{2,1,0:T(8,128)} async-done(((f32[2,512,1024]{2,1,0:T(8,128)}), f32[2,512,256]{2,1,0:T(8,128)}) %reduce-scatter.2.cloned.1.call-update) | async-done | bytes 1048592 | tf_op jit(solution)/shard_map/reduce_scatter | solution.py:68
  117.9 2.3 %fusion.26 = (f32[2,512,256]{2,1,0:T(8,128)S(1)}, f32[2,512,256]{2,1,0:T(8,128)}) fusion(f32[2,512,256]{2,1,0:T(8,128)} %reduce-scatter.2.cloned.1.call-done, pred[512]{0:T(512)(128)(4,1)S(1)} %broadcast_in_dim.53), kind=kLoop, calls=%fused_computation.59 | loop fusion | flops 524288 | bytes 3146240 | tf_op jit(solution)/shard_map/neg | solution.py:76
  120.5 1.0 fusion.19
  121.5 1.0 fusion.20
  122.5 1.0 fusion.10
  123.5 1.0 fusion.11
  124.5 0.8 pad_maximum_fusion
  125.4 37.0 %all-reduce.2.cloned.1.call-done = f32[2,1,256,256]{3,2,1,0:T(8,128)} async-done(((f32[2,1,256,256]{3,2,1,0:T(8,128)}), f32[2,1,256,256]{3,2,1,0:T(8,128)}) %all-reduce.2.cloned.1.call-update) | async-done | bytes 524304 | tf_op jit(solution)/shard_map/psum | solution.py:84
  162.4 1.9 %sub.26 = f32[2,1,256,256]{3,2,1,0:T(8,128)} subtract(f32[2,1,256,256]{3,2,1,0:T(8,128)S(1)} %copy-done.2, f32[2,1,256,256]{3,2,1,0:T(8,128)} %all-reduce.2.cloned.1.call-done) | non-fusion elementwise | flops 131072 | bytes 1572864 | tf_op jit(solution)/shard_map/sub | solution.py:85
  (48 shorter events, 5.7 us)
Async XLA Ops:
  7.2 34.7 %copy-start = (bf16[2,4,256,256]{3,2,1,0:T(8,128)(2,1)S(1)}, bf16[2,4,256,256]{3,2,1,0:T(8,128)(2,1)}, u32[]{:S(2)}) copy-start(bf16[2,4,256,256]{3,2,1,0:T(8,128)(2,1)} %param.9) | copy-start | bytes 3145732
  7.2 33.1 %all-gather.2.cloned.1.call-start = ((), (), s32[]{:S(2)}) async-start(), calls=%async_computation.2 | async-start | bytes 1310720 | tf_op jit(solution)/shard_map/all_gather | solution.py:34
  7.9 110.0 %reduce-scatter.2.cloned.1.call-start = ((), (), s32[]{:S(2)}) async-start(), calls=%async_computation.3 | async-start | bytes 5242880 | tf_op jit(solution)/shard_map/reduce_scatter | solution.py:68
  40.3 3.0 %copy-start.1 = (bf16[2,4,256,256]{3,2,1,0:T(8,128)(2,1)S(1)}, bf16[2,4,256,256]{3,2,1,0:T(8,128)(2,1)}, u32[]{:S(2)}) copy-start(bf16[2,4,256,256]{3,2,1,0:T(8,128)(2,1)} %all-gather.2.cloned.1.call-done) | copy-start | bytes 3145732
  64.5 41.6 %all-to-all-start = ((bf16[2,4,512,256]{3,2,0,1:T(8,128)(2,1)}), bf16[2,4,512,256]{3,2,0,1:T(8,128)(2,1)S(1)}, u32[]{:S(2)}, u32[]{:S(2)}) async-start(bf16[2,4,512,256]{3,2,0,1:T(8,128)(2,1)} %copy.17), calls=%async_computation.1 | async-start | bytes 4194304 | tf_op jit(solution)/shard_map/all_to_all | solution.py:79
  68.2 94.1 %all-reduce.2.cloned.1.call-start = ((), (), s32[]{:S(2)}) async-start(), calls=%async_computation.4 | async-start | bytes 1048576 | tf_op jit(solution)/shard_map/psum | solution.py:84
  120.4 41.9 %copy-start.2 = (f32[2,1,256,256]{3,2,1,0:T(8,128)S(1)}, f32[2,1,256,256]{3,2,1,0:T(8,128)}, u32[]{:S(2)}) copy-start(f32[2,1,256,256]{3,2,1,0:T(8,128)} %param.10) | copy-start | bytes 1572868
Sparse Core Ops, SparseCore 0:
  9.6 30.6 all-gather.1
  62.4 55.4 reduce-scatter.1
  125.5 36.8 all-reduce.1
where the time goes:
time: 171 us
  waiting for transfers between devices  115 us (67%)
  matrix products  16.1 us (9%)
  between operations  13.9 us (8%)
  other arithmetic  12.6 us (7%)
  local copies, waits for them, and re-layouts  8.88 us (5%)
  starting transfers between devices  3.88 us (2%)
    psum x1, waiting for transfers between devices, local(): total_sum = lax.psum(quad_term, 'prow')  37 us
    all_to_all x1, waiting for transfers between devices, local(): lax.all_to_all(z_rows, 'pcol', split_axis=1, concat_axis=1, tiled=True)  36.9 us
    all_gather x1, waiting for transfers between devices, local(): rows_in = lax.all_gather(panel, 'prow', axis=2, tiled=True)  29.1 us
    reduce_scatter x1, waiting for transfers between devices, local(): lax.psum_scatter(partial_value.reshape(2, rows_all, total_k * block_width...  11.5 us
    dot_general x4, matrix products, one_node(): jnp.einsum('sg,cigw->cisw', table_k, ainv_blocks, preferred_element_type=...  4.94 us
    reshape x1, local copies, waits for them, and re-layouts, local(): partial_value.reshape(2, rows_all, total_k * block_width)  4.76 us
    dynamic_update_slice x4, other arithmetic, local(): per_node = lax.map(one_node, (pick_table, jnp.moveaxis(placed, 1, 0)))  4.27 us
    dot_general x4, matrix products, single(): return jnp.einsum('kra,rkb->kab', left, right, precision=highest)  4.02 us
  transfers between devices with their start and end apart: 4, of which 4 were waited for; matrix products, arithmetic and copies ran while one was open for 4% of the time, Pallas kernels for 0%

commit v1 on v0

--- a/solution.py
+++ b/solution.py
@@ -31,7 +31,12 @@
     slot_pos = col_struct - col_here * group_blocks
     first_block = row_here * row_blocks
     target = first_block + jnp.arange(row_blocks, dtype=jnp.int32)
-    rows_in = lax.all_gather(panel, "prow", axis=2, tiled=True)
+    ring = [panel]
+    for hop in range(3):
+        ring.append(lax.ppermute(ring[-1], "prow", [(dev, (dev + 1) % 4) for dev in range(4)]))
+    rows_in = jnp.roll(
+        jnp.concatenate(ring[::-1], axis=2), (lax.axis_index("prow") + 1) * ring[0].shape[2], axis=2
+    )
 
     def single(left, right):
         return jnp.einsum("knb,kbc->knc", left, right, preferred_element_type=jnp.float32)

time: 171 us -> 164 us (0.959)
  waiting for transfers between devices: 115 us -> 109 us
  starting transfers between devices: 3.88 us -> 6.8 us
  matrix products: 16.1 us -> 13.8 us
    all_gather x1 -> x0, waiting for transfers between devices: 29.1 us -> none  [local(): rows_in = lax.all_gather(panel, 'prow', axis=2, tiled=True)]
    ppermute x0 -> x3, waiting for transfers between devices: none -> 24.4 us  [local(): lax.ppermute(ring[-1], 'prow', [(dev, (dev + 1) % 4) for dev in range(4)])]
    ppermute x0 -> x3, starting transfers between devices: none -> 3.11 us  [local(): lax.ppermute(ring[-1], 'prow', [(dev, (dev + 1) % 4) for dev in range(4)])]
    dot_general x4, matrix products: 3.53 us -> 1.21 us  [single(): jnp.einsum('knb,kbc->knc', left, right, preferred_element_type=jnp.float32)]
    all_to_all x1, waiting for transfers between devices: 36.9 us -> 39.1 us  [local(): lax.all_to_all(z_rows, 'pcol', split_axis=1, concat_axis=1, tiled=True)]
  transfers between devices with their start and end apart: 4 -> 6, of which waited for: 4 -> 6; matrix products, arithmetic and copies ran while one was open for 4% -> 3% of each run, Pallas kernels for 0% -> 0%
where the time goes in v1:
time: 164 us
  waiting for transfers between devices  109 us (66%)
  between operations  14.3 us (9%)
  matrix products  13.8 us (8%)
  other arithmetic  11.2 us (7%)
  local copies, waits for them, and re-layouts  8.37 us (5%)
  starting transfers between devices  6.8 us (4%)
    all_to_all x1, waiting for transfers between devices, local(): lax.all_to_all(z_rows, 'pcol', split_axis=1, concat_axis=1, tiled=True)  39.1 us
    psum x1, waiting for transfers between devices, local(): total_sum = lax.psum(quad_term, 'prow')  35.5 us
    ppermute x3, waiting for transfers between devices, local(): lax.ppermute(ring[-1], 'prow', [(dev, (dev + 1) % 4) for dev in range(4)])  24.4 us
    reduce_scatter x1, waiting for transfers between devices, local(): lax.psum_scatter(partial_value.reshape(2, rows_all, total_k * block_width...  10 us
    dot_general x4, matrix products, one_node(): jnp.einsum('sg,cigw->cisw', table_k, ainv_blocks, preferred_element_type=...  4.93 us
    reshape x1, local copies, waits for them, and re-layouts, local(): partial_value.reshape(2, rows_all, total_k * block_width)  4.76 us
    dynamic_update_slice x4, other arithmetic, local(): per_node = lax.map(one_node, (pick_table, jnp.moveaxis(placed, 1, 0)))  4.27 us
    dot_general x4, matrix products, single(): return jnp.einsum('kra,rkb->kab', left, right, precision=highest)  4.02 us
  transfers between devices with their start and end apart: 6, of which 6 were waited for; matrix products, arithmetic and copies ran while one was open for 3% of the time, Pallas kernels for 0%

profile of v1, /device:TPU:0, one launch (start us, length us, event | category | flops | bytes accessed | tf_op | source)
XLA Modules:
  0.0 163.7 jit_solution(1893315024322632537)
XLA Ops:
  7.2 3.1 %collective-permute-start = (bf16[2,4,64,256]{3,2,1,0:T(8,128)(2,1)}, bf16[2,4,64,256]{3,2,1,0:T(8,128)(2,1)S(1)}, u32[]{:S(2)}, u32[]{:S(2)}) collective-permute-start(bf16[2,4,64,256]{3,2,1,0:T(8,128)(2,1)} %param.8), channel_id=1, source_target_pairs={{0,4},{4,8},{8,12},{12,0},{1,5},{5,9},{9,13},{13,1},{2,6},{6,10},{... | collective-permute-start | bytes 786440 | tf_op jit(solution)/shard_map/ppermute | solution.py:36
  10.3 8.5 %collective-permute-done = bf16[2,4,64,256]{3,2,1,0:T(8,128)(2,1)S(1)} collective-permute-done((bf16[2,4,64,256]{3,2,1,0:T(8,128)(2,1)}, bf16[2,4,64,256]{3,2,1,0:T(8,128)(2,1)S(1)}, u32[]{:S(2)}, u32[]{:S(2)}) %collective-permute-start) | collective-permute-done | bytes 262176 | tf_op jit(solution)/shard_map/ppermute | solution.py:36
  18.9 9.3 %collective-permute-done.1 = bf16[2,4,64,256]{3,2,1,0:T(8,128)(2,1)S(1)} collective-permute-done((bf16[2,4,64,256]{3,2,1,0:T(8,128)(2,1)S(1)}, bf16[2,4,64,256]{3,2,1,0:T(8,128)(2,1)S(1)}, u32[]{:S(2)}, u32[]{:S(2)}) %collective-permute-start.1) | collective-permute-done | bytes 262176 | tf_op jit(solution)/shard_map/ppermute | solution.py:36
  28.1 1.3 reshape.276
  30.0 6.6 %collective-permute-done.2 = bf16[2,4,64,256]{3,2,1,0:T(8,128)(2,1)S(1)} collective-permute-done((bf16[2,4,64,256]{3,2,1,0:T(8,128)(2,1)S(1)}, bf16[2,4,64,256]{3,2,1,0:T(8,128)(2,1)S(1)}, u32[]{:S(2)}, u32[]{:S(2)}) %collective-permute-start.2) | collective-permute-done | bytes 262176 | tf_op jit(solution)/shard_map/ppermute | solution.py:36
  36.8 0.3 fusion.14
  37.1 0.3 fusion.16
  37.4 0.3 fusion.8
  37.7 0.3 fusion.9
  38.2 13.5 %while.10 = (s32[]{:T(128)}, f32[4,2,512,256]{3,2,1,0:T(8,128)}, bf16[4,1,2]{2,1,0:T(2,128)(2,1)S(1)}, bf16[2,512,2,256]{3,2,1,0:T(2,128)(2,1)S(1)}, bf16[4,2,1,256,256]{4,3,0,2,1:T(8,128)(2,1)S(1)}, /*index=5*/s32[]{:T(128)}) while((s32[]{:T(128)}, f32[4,2,512,256]{3,2,1,0:T(8,128)}, bf16[4,1,2]{2,1,0:T(2,128)(2,1)S(1)}, ...), condition=%wide.region_2.3_spmd, body=%wide.region_1.2_spmd.sunk | while | flops 270008320 | bytes 9962573 | solution.py:68
  38.2 1.2 fusion.47
  40.5 1.0 fusion.52
  41.6 1.2 fusion.47
  43.9 1.1 fusion.52
  45.0 1.2 fusion.47
  47.3 1.1 fusion.52
  48.3 1.2 fusion.47
  50.6 1.0 fusion.52
  51.7 4.8 %copy.21 = f32[4,2,64,8,256]{4,3,0,2,1:T(8,128)} copy(f32[4,2,64,8,256]{4,3,2,1,0:T(8,128)} %bitcast.36) | data formatting | bytes 8388608 | tf_op jit(solution)/shard_map/reshape | solution.py:74
  56.8 0.5 multiply_convert_fusion
  57.2 1.5 copy.17
  58.7 3.6 %all-to-all-start = ((bf16[2,4,512,256]{3,2,0,1:T(8,128)(2,1)}), bf16[2,4,512,256]{3,2,0,1:T(8,128)(2,1)S(1)}, u32[]{:S(2)}, u32[]{:S(2)}) async-start(bf16[2,4,512,256]{3,2,0,1:T(8,128)(2,1)} %copy.17), calls=%async_computation.1 | async-start | bytes 4194304 | tf_op jit(solution)/shard_map/all_to_all | solution.py:84
  62.6 39.1 %all-to-all-done = bf16[2,4,512,256]{3,2,0,1:T(8,128)(2,1)S(1)} async-done(((bf16[2,4,512,256]{3,2,0,1:T(8,128)(2,1)}), bf16[2,4,512,256]{3,2,0,1:T(8,128)(2,1)S(1)}, u32[]{:S(2)}, u32[]{:S(2)}) %all-to-all-start) | async-done | bytes 2097184 | tf_op jit(solution)/shard_map/all_to_all | solution.py:84
  102.0 10.0 %reduce-scatter.2.cloned.1.call-done = f32[2,512,256]{2,1,0:T(8,128)} async-done(((f32[2,512,1024]{2,1,0:T(8,128)}), f32[2,512,256]{2,1,0:T(8,128)}) %reduce-scatter.2.cloned.1.call-update) | async-done | bytes 1048592 | tf_op jit(solution)/shard_map/reduce_scatter | solution.py:73
  111.9 2.3 %fusion.31 = (f32[2,512,256]{2,1,0:T(8,128)S(1)}, f32[2,512,256]{2,1,0:T(8,128)}) fusion(f32[2,512,256]{2,1,0:T(8,128)} %reduce-scatter.2.cloned.1.call-done, pred[512]{0:T(512)(128)(4,1)S(1)} %broadcast_in_dim.53), kind=kLoop, calls=%fused_computation.72 | loop fusion | flops 524288 | bytes 3146240 | tf_op jit(solution)/shard_map/neg | solution.py:81
  114.5 1.0 fusion.20
  115.5 1.0 fusion.19
  116.6 1.0 fusion.11
  117.6 1.0 fusion.10
  118.6 0.8 pad_maximum_fusion
  119.5 35.5 %all-reduce.2.cloned.1.call-done = f32[2,1,256,256]{3,2,1,0:T(8,128)} async-done(((f32[2,1,256,256]{3,2,1,0:T(8,128)}), f32[2,1,256,256]{3,2,1,0:T(8,128)}) %all-reduce.2.cloned.1.call-update) | async-done | bytes 524304 | tf_op jit(solution)/shard_map/psum | solution.py:89
  155.0 1.9 %sub.31 = f32[2,1,256,256]{3,2,1,0:T(8,128)} subtract(f32[2,1,256,256]{3,2,1,0:T(8,128)S(1)} %copy-done.2, f32[2,1,256,256]{3,2,1,0:T(8,128)} %all-reduce.2.cloned.1.call-done) | non-fusion elementwise | flops 131072 | bytes 1572864 | tf_op jit(solution)/shard_map/sub | solution.py:90
  (61 shorter events, 6.0 us)
Async XLA Ops:
  7.2 29.5 %copy-start.1 = (bf16[2,4,64,256]{3,2,1,0:T(8,128)(2,1)S(1)}, bf16[2,4,64,256]{3,2,1,0:T(8,128)(2,1)}, u32[]{:S(2)}) copy-start(bf16[2,4,64,256]{3,2,1,0:T(8,128)(2,1)} %param.8) | copy-start | bytes 786436
  7.2 22.3 %copy-start.3 = (s32[4,4]{1,0:T(4,128)S(1)}, s32[4,4]{1,0:T(4,128)}, u32[]{:S(2)}) copy-start(s32[4,4]{1,0:T(4,128)} %param.11) | copy-start | bytes 196
  7.2 104.8 %reduce-scatter.2.cloned.1.call-start = ((), (), s32[]{:S(2)}) async-start(), calls=%async_computation.2 | async-start | bytes 5242880 | tf_op jit(solution)/shard_map/reduce_scatter | solution.py:73
  7.2 11.6 %collective-permute-start = (bf16[2,4,64,256]{3,2,1,0:T(8,128)(2,1)}, bf16[2,4,64,256]{3,2,1,0:T(8,128)(2,1)S(1)}, u32[]{:S(2)}, u32[]{:S(2)}) collective-permute-start(bf16[2,4,64,256]{3,2,1,0:T(8,128)(2,1)} %param.8), channel_id=1, source_target_pairs={{0,4},{4,8},{8,12},{12,0},{1,5},{5,9},{9,13},{13,1},{2,6},{6,10},{... | collective-permute-start | bytes 786440 | tf_op jit(solution)/shard_map/ppermute | solution.py:36
  18.9 9.3 %collective-permute-start.1 = (bf16[2,4,64,256]{3,2,1,0:T(8,128)(2,1)S(1)}, bf16[2,4,64,256]{3,2,1,0:T(8,128)(2,1)S(1)}, u32[]{:S(2)}, u32[]{:S(2)}) collective-permute-start(bf16[2,4,64,256]{3,2,1,0:T(8,128)(2,1)S(1)} %collective-permute-done), channel_id=1, source_target_pairs={{0,4},{4,8},{8,12},{12,0},{1,5},{5,9},{9,13},{13,1},{2,6},{6,10},{... | collective-permute-start | bytes 786440 | tf_op jit(solution)/shard_map/ppermute | solution.py:36
  28.1 8.4 %collective-permute-start.2 = (bf16[2,4,64,256]{3,2,1,0:T(8,128)(2,1)S(1)}, bf16[2,4,64,256]{3,2,1,0:T(8,128)(2,1)S(1)}, u32[]{:S(2)}, u32[]{:S(2)}) collective-permute-start(bf16[2,4,64,256]{3,2,1,0:T(8,128)(2,1)S(1)} %collective-permute-done.1), channel_id=1, source_target_pairs={{0,4},{4,8},{8,12},{12,0},{1,5},{5,9},{9,13},{13,1},{2,6},{6,10},{... | collective-permute-start | bytes 786440 | tf_op jit(solution)/shard_map/ppermute | solution.py:36
  30.0 6.8 %copy-start = (bf16[2,4,256,256]{3,2,1,0:T(8,128)(2,1)S(1)}, bf16[2,4,256,256]{3,2,1,0:T(8,128)(2,1)}, u32[]{:S(2)}) copy-start(bf16[2,4,256,256]{3,2,1,0:T(8,128)(2,1)} %param.9) | copy-start | bytes 3145732
  58.7 42.9 %all-to-all-start = ((bf16[2,4,512,256]{3,2,0,1:T(8,128)(2,1)}), bf16[2,4,512,256]{3,2,0,1:T(8,128)(2,1)S(1)}, u32[]{:S(2)}, u32[]{:S(2)}) async-start(bf16[2,4,512,256]{3,2,0,1:T(8,128)(2,1)} %copy.17), calls=%async_computation.1 | async-start | bytes 4194304 | tf_op jit(solution)/shard_map/all_to_all | solution.py:84
  62.3 92.6 %all-reduce.2.cloned.1.call-start = ((), (), s32[]{:S(2)}) async-start(), calls=%async_computation.3 | async-start | bytes 1048576 | tf_op jit(solution)/shard_map/psum | solution.py:89
  116.6 38.4 %copy-start.2 = (f32[2,1,256,256]{3,2,1,0:T(8,128)S(1)}, f32[2,1,256,256]{3,2,1,0:T(8,128)}, u32[]{:S(2)}) copy-start(f32[2,1,256,256]{3,2,1,0:T(8,128)} %param.10) | copy-start | bytes 1572868
Sparse Core Ops, SparseCore 0:
  56.6 55.3 reduce-scatter.1
  119.6 35.3 all-reduce.1
